TPU v7x, 32 devices: a whole 2x2x4 slice. The times are simulated.
32 devices in a mesh: chan: 4 (over x, core), slab: 8 (over z, y).
Axes of the slice: x: 2, y: 2, z: 4, core: 2. Of those that a mesh axis runs over, the one named last changes fastest.
Arguments:
- beam_images: float32 [64, 512, 4096], P('chan', 'slab'), may hold values from -24 to 24
- chan_weights: int32 [64], P('chan'), may hold values from 1 to 8
- freq_offsets: float32 [64], P('chan'), may hold values from -1 to 1
- half_widths: int32 [5], replicated, may hold values from 16 to 32, as said below
Outputs:
- smoothed: float32 [5, 512, 4096], P(None, 'slab', 'chan')
Inputs may be any that keep to these rules, and one draw needn't show every extreme that they name: `half_widths`: each half-width is at least 16 and at most 32; at least one equals 32.
All inputs are finite; a program needn't handle non-finite values.
Results may differ from a plain program's by a relative error of at most 0.00008.
Values sent between devices are 32-bit elements; how exact they have to be, the bound alone decides.
A program may use at most 128 MiB of HBM per device.

v0:
```python
import functools

import jax
import jax.numpy as jnp
from jax import lax
from jax.experimental import pallas as pl
from jax.experimental.pallas import tpu as pltpu
from jax.sharding import PartitionSpec as P

MOMENTS = 5
HW_MAX = 32
LANES = 128
STEP = 2 * LANES
PARTS = 2
ROWS_AT_ONCE = 32
MESH = pl.DeviceIdType.MESH


def split(value):
    parts = []
    for _ in range(PARTS - 1):
        part = value.astype(jnp.bfloat16)
        parts.append(part)
        value = value - part.astype(jnp.float32)
    parts.append(value.astype(jnp.bfloat16))
    return parts


def kernel(
    chans, slabs,
    w_ref, f_ref, h_ref, beam_ref, out_ref,
    beams, pieces, band, row_band, sums, passed, crossed, ext, weights,
    load_sem, pass_send, pass_recv, cross_send, cross_recv,
    up_send, up_recv, down_send, down_recv, w_send, w_recv,
):
    groups = chans // 2
    me = lax.axis_index("chan")
    slab = lax.axis_index("slab")
    group, core = me // 2, lax.rem(me, 2)
    local_chans, rows, all_cols = beam_ref.shape
    width = all_cols // chans
    steps = width // STEP
    tiles = width // LANES + 2
    chunks = width // LANES
    partner = group * 2 + (1 - core)
    not_first, not_last = slab > 0, slab < slabs - 1

    def block_of(slot):
        owner_group = lax.rem(group + slot // 2 + 1, groups)
        return owner_group * 2 + (1 - core if slot % 2 == 0 else core)

    def tile_col(slot, tile):
        return block_of(slot) * width + (tile - 1) * LANES

    def load(slot, tile):
        col = pl.multiple_of(tile_col(slot, tile), LANES)
        return pltpu.make_async_copy(
            beam_ref.at[:, :, pl.ds(col, LANES)], beams.at[slot, tile], load_sem.at[slot, tile]
        )

    def inside(slot, tile):
        col = tile_col(slot, tile)
        return jnp.logical_and(col >= 0, col < all_cols)

    def start_load(slot, tile):
        @pl.when(inside(slot, tile))
        def _():
            load(slot, tile).start()

    for slot in range(chans):
        @pl.loop(0, 4)
        def _(tile):
            start_load(slot, tile)

    @pl.loop(4, tiles)
    def _(tile):
        for slot in range(chans):
            start_load(slot, tile)

    barrier = pltpu.get_barrier_semaphore()
    for offset in range(1, chans):
        pl.semaphore_signal(
            barrier, inc=1, device_id={"chan": lax.rem(me + offset, chans)}, device_id_type=MESH
        )

    @pl.when(not_first)
    def _():
        pl.semaphore_signal(barrier, inc=1, device_id={"slab": slab - 1}, device_id_type=MESH)

    @pl.when(not_last)
    def _():
        pl.semaphore_signal(barrier, inc=1, device_id={"slab": slab + 1}, device_id_type=MESH)

    total = w_ref[0].astype(jnp.float32)
    for chan in range(1, local_chans):
        total = total + w_ref[chan].astype(jnp.float32)
    weights[0] = jnp.full(weights.shape[1:], total, jnp.float32)

    @pl.loop(0, MOMENTS)
    def _(k):
        reach = h_ref[k]
        for at in range(0, 2 * STEP, LANES):
            source = lax.broadcasted_iota(jnp.int32, (LANES, STEP), 0) + at
            target = lax.broadcasted_iota(jnp.int32, (LANES, STEP), 1)
            near = jnp.abs(source - LANES - target) <= reach
            band[k, at : at + LANES, :] = jnp.where(near, 1.0, 0.0).astype(jnp.bfloat16)
        span = rows + 2 * HW_MAX
        target = lax.broadcasted_iota(jnp.int32, (rows, span), 0)
        source = lax.broadcasted_iota(jnp.int32, (rows, span), 1)
        near = jnp.abs(source - HW_MAX - target) <= reach
        near = jnp.where(near, 1.0, 0.0).astype(jnp.bfloat16)
        for part in range(PARTS):
            row_band[k, :, part * span : (part + 1) * span] = near

    @pl.when(slab == 0)
    def _():
        @pl.loop(0, chunks)
        def _(i):
            ext[i, :, 0:HW_MAX, :] = jnp.zeros((MOMENTS, HW_MAX, LANES), jnp.float32)

    @pl.when(slab == slabs - 1)
    def _():
        @pl.loop(0, chunks)
        def _(i):
            ext[i, :, HW_MAX + rows :, :] = jnp.zeros((MOMENTS, HW_MAX, LANES), jnp.float32)

    pl.semaphore_wait(
        barrier, chans - 1 + not_first.astype(jnp.int32) + not_last.astype(jnp.int32)
    )

    def weight_copy(offset):
        return pltpu.make_async_remote_copy(
            src_ref=weights.at[0], dst_ref=weights.at[offset],
            send_sem=w_send.at[offset - 1], recv_sem=w_recv.at[offset - 1],
            device_id={"chan": lax.rem(me + offset, chans)}, device_id_type=MESH,
        )

    def pass_copy(hop, j):
        return pltpu.make_async_remote_copy(
            src_ref=sums.at[2 * hop, pl.ds(2 * j, 2)], dst_ref=passed.at[hop, pl.ds(2 * j, 2)],
            send_sem=pass_send.at[hop, j], recv_sem=pass_recv.at[hop, j],
            device_id={"chan": partner}, device_id_type=MESH,
        )

    def cross_copy(hop, i):
        other = lax.rem(group + hop + 1, groups) * 2 + core
        return pltpu.make_async_remote_copy(
            src_ref=sums.at[2 * hop + 1, i], dst_ref=crossed.at[hop, i],
            send_sem=cross_send.at[hop, i], recv_sem=cross_recv.at[hop, i],
            device_id={"chan": other}, device_id_type=MESH,
        )

    def up_copy(i):
        return pltpu.make_async_remote_copy(
            src_ref=ext.at[i, :, pl.ds(HW_MAX, HW_MAX)],
            dst_ref=ext.at[i, :, pl.ds(HW_MAX + rows, HW_MAX)],
            send_sem=up_send.at[i], recv_sem=up_recv.at[i],
            device_id={"slab": slab - 1}, device_id_type=MESH,
        )

    def down_copy(i):
        return pltpu.make_async_remote_copy(
            src_ref=ext.at[i, :, pl.ds(rows, HW_MAX)],
            dst_ref=ext.at[i, :, pl.ds(0, HW_MAX)],
            send_sem=down_send.at[i], recv_sem=down_recv.at[i],
            device_id={"slab": slab + 1}, device_id_type=MESH,
        )

    for offset in range(1, chans):
        weight_copy(offset).start()

    def moments_of(slot, tile):
        valid = inside(slot, tile)

        @pl.when(valid)
        def _():
            load(slot, tile).wait()

        @pl.when(jnp.logical_not(valid))
        def _():
            beams[slot, tile] = jnp.zeros(beams.shape[2:], jnp.float32)

        cols = pl.ds(pl.multiple_of(tile * LANES, LANES), LANES)

        @pl.loop(0, rows // ROWS_AT_ONCE)
        def _(part):
            first = pl.multiple_of(part * ROWS_AT_ONCE, ROWS_AT_ONCE)
            totals = [None] * MOMENTS
            for chan in range(local_chans):
                weight = w_ref[chan].astype(jnp.float32)
                offset = f_ref[chan]
                term = beams[slot, tile, chan, pl.ds(first, ROWS_AT_ONCE), :] * weight
                for k in range(MOMENTS):
                    if k > 0:
                        term = term * offset
                    totals[k] = term if chan == 0 else totals[k] + term
            for k in range(MOMENTS):
                for at, piece in enumerate(split(totals[k])):
                    pieces[slot, k, pl.ds(first + at * rows, ROWS_AT_ONCE), cols] = piece

    def columns_of(slot, j):
        wide = pl.ds(pl.multiple_of(j * STEP, STEP), 2 * STEP)

        for k in range(MOMENTS):
            product = jnp.dot(
                pieces[slot, k, :, wide], band[k], preferred_element_type=jnp.float32
            )
            result = product[:rows]
            for at in range(1, PARTS):
                result = result + product[at * rows : (at + 1) * rows]
            sums[slot, 2 * j, k] = result[:, :LANES]
            sums[slot, 2 * j + 1, k] = result[:, LANES:]

    def step(j, first_tile, last_tile, hops):
        def make(slot):
            @pl.loop(first_tile, last_tile)
            def _(tile):
                moments_of(slot, tile)

            columns_of(slot, j)

        for hop in hops:
            make(2 * hop)
            pass_copy(hop, j).start()
            make(2 * hop + 1)
            pass_copy(hop, j).wait_recv()
            for half in range(2):
                i = 2 * j + half
                sums[2 * hop + 1, i] = sums[2 * hop + 1, i] + passed[hop, i]
                if hop < groups - 1:
                    cross_copy(hop, i).start()

    def finish(i):
        value = sums[chans - 1, i]
        for hop in range(groups - 1):
            cross_copy(hop, i).wait_recv()
            value = value + crossed[hop, i]
        ext[i, :, HW_MAX : HW_MAX + rows, :] = value

        @pl.when(not_first)
        def _():
            up_copy(i).start()

        @pl.when(not_last)
        def _():
            down_copy(i).start()

    def rows_of(i):
        @pl.when(not_last)
        def _():
            up_copy(i).wait_recv()

        @pl.when(not_first)
        def _():
            down_copy(i).wait_recv()

        weight_total = weights[0]
        for offset in range(1, chans):
            weight_total = weight_total + weights[offset]
        for k in range(MOMENTS):
            both = jnp.concatenate(split(ext[i, k]), axis=0)
            summed = jnp.dot(row_band[k], both, preferred_element_type=jnp.float32)
            divisor = weight_total * (2 * h_ref[k] + 1).astype(jnp.float32)
            out_ref[k, :, pl.ds(pl.multiple_of(i * LANES, LANES), LANES)] = (
                summed * (1.0 / divisor)[0:1, :]
            )

    step(0, 0, 4, range(groups))

    @pl.loop(1, steps)
    def _(j):
        step(j, 2 * j + 2, 2 * j + 4, range(groups - 1))
        finish(j - 1)
        step(j, 2 * j + 2, 2 * j + 4, range(groups - 1, groups))

    for offset in range(1, chans):
        weight_copy(offset).wait_recv()

    @pl.loop(steps - 1, chunks)
    def _(i):
        finish(i)

        @pl.when(i == steps - 1)
        def _():
            @pl.loop(0, steps - 3)
            def _(late):
                rows_of(late)

        rows_of(i - 2)

    @pl.loop(chunks - 2, chunks)
    def _(i):
        rows_of(i)

    for offset in range(1, chans):
        weight_copy(offset).wait_send()

    @pl.loop(0, steps)
    def _(j):
        for hop in range(groups):
            pass_copy(hop, j).wait_send()

    @pl.loop(0, chunks)
    def _(i):
        for hop in range(groups - 1):
            cross_copy(hop, i).wait_send()

        @pl.when(not_first)
        def _():
            up_copy(i).wait_send()

        @pl.when(not_last)
        def _():
            down_copy(i).wait_send()


def body(chans, slabs, beam_images, chan_weights, freq_offsets, half_widths):
    local_chans, rows, all_cols = beam_images.shape
    width = all_cols // chans
    chunks, steps, tiles, groups = width // LANES, width // STEP, width // LANES + 2, chans // 2
    f32, b16 = jnp.float32, jnp.bfloat16
    dma = pltpu.SemaphoreType.DMA
    smem = pl.BlockSpec(memory_space=pltpu.SMEM)
    anywhere = pl.BlockSpec(memory_space=pl.ANY)
    span = rows + 2 * HW_MAX
    return pl.pallas_call(
        functools.partial(kernel, chans, slabs),
        out_shape=jax.ShapeDtypeStruct((MOMENTS, rows, width), f32),
        in_specs=[smem, smem, smem, anywhere],
        out_specs=pl.BlockSpec(memory_space=pltpu.VMEM),
        scratch_shapes=[
            pltpu.VMEM((chans, tiles, local_chans, rows, LANES), f32),
            pltpu.VMEM((chans, MOMENTS, PARTS * rows, tiles * LANES), b16),
            pltpu.VMEM((MOMENTS, 2 * STEP, STEP), b16),
            pltpu.VMEM((MOMENTS, rows, PARTS * span), b16),
            pltpu.VMEM((chans, chunks, MOMENTS, rows, LANES), f32),
            pltpu.VMEM((groups, chunks, MOMENTS, rows, LANES), f32),
            pltpu.VMEM((groups - 1, chunks, MOMENTS, rows, LANES), f32),
            pltpu.VMEM((chunks, MOMENTS, span, LANES), f32),
            pltpu.VMEM((chans, 8, LANES), f32),
            dma((chans, tiles)),
            dma((groups, steps)),
            dma((groups, steps)),
            dma((groups - 1, chunks)),
            dma((groups - 1, chunks)),
            dma((chunks,)),
            dma((chunks,)),
            dma((chunks,)),
            dma((chunks,)),
            dma((chans - 1,)),
            dma((chans - 1,)),
        ],
        compiler_params=pltpu.CompilerParams(
            collective_id=0, has_side_effects=True, vmem_limit_bytes=44 * 1024 * 1024
        ),
    )(chan_weights, freq_offsets, half_widths, beam_images)


def solution(mesh):
    placed = (P("chan", "slab", None), P("chan"), P("chan"), P())
    return jax.shard_map(
        functools.partial(body, mesh.shape["chan"], mesh.shape["slab"]),
        mesh=mesh, in_specs=placed, out_specs=P(None, "slab", "chan"), check_vma=False,
    )
```

profile of v0, /device:TPU:9, one launch (start us, length us, event | category | flops | bytes accessed | tf_op | source)
XLA Modules:
  0.0 48.3 jit_solution(9795238095603936842)
XLA Ops:
  0.0 0.0 copy-start
  0.0 0.7 %copy-done = s32[16]{0:T(128)S(1)} copy-done((s32[16]{0:T(128)S(1)}, s32[16]{0:T(128)}, u32[]{:S(2)}) %copy-start) | copy-done | bytes 88
  0.7 0.0 copy-start.1
  0.7 0.7 %copy-done.1 = f32[16]{0:T(128)S(1)} copy-done((f32[16]{0:T(128)S(1)}, f32[16]{0:T(128)}, u32[]{:S(2)}) %copy-start.1) | copy-done | bytes 88
  1.3 0.0 copy-start.2
  1.3 0.7 %copy-done.2 = s32[5]{0:T(128)S(1)} copy-done((s32[5]{0:T(128)S(1)}, s32[5]{0:T(128)}, u32[]{:S(2)}) %copy-start.2) | copy-done | bytes 44
  2.0 45.3 %shard_map.46 = f32[5,64,1024]{2,1,0:T(8,128)S(1)} custom-call(s32[16]{0:T(128)S(1)} %copy-done, f32[16]{0:T(128)S(1)} %copy-done.1, s32[5]{0:T(128)S(1)} %copy-done.2, f32[16,64,4096]{2,1,0:T(8,128)} %beam_ref.1), custom_call_target="tpu_custom_call" | custom-call | tf_op jit(solution)/shard_map/pallas_call | solution.py:326
  47.2 1.1 %copy.6 = f32[5,64,1024]{2,1,0:T(8,128)} copy(f32[5,64,1024]{2,1,0:T(8,128)S(1)} %shard_map.46) | data formatting | bytes 2621440
Async XLA Ops:
  0.0 0.7 %copy-start = (s32[16]{0:T(128)S(1)}, s32[16]{0:T(128)}, u32[]{:S(2)}) copy-start(s32[16]{0:T(128)} %w_ref.1) | copy-start | bytes 196
  0.7 0.7 %copy-start.1 = (f32[16]{0:T(128)S(1)}, f32[16]{0:T(128)}, u32[]{:S(2)}) copy-start(f32[16]{0:T(128)} %f_ref.1) | copy-start | bytes 196
  1.3 0.7 %copy-start.2 = (s32[5]{0:T(128)S(1)}, s32[5]{0:T(128)}, u32[]{:S(2)}) copy-start(s32[5]{0:T(128)} %h_ref.1) | copy-start | bytes 64
where the time goes:
time: 48.5 us; the launch traced here: 48.3 us
  Pallas kernels  45.3 us (93%)
  local copies, waits for them, and re-layouts  3.02 us (6%)
    pallas_call x1, Pallas kernels, body(): pl.pallas_call(functools.partial(kernel, chans, slabs), out_shape=jax.Sha...  45.3 us
    unnamed x7, local copies, waits for them, and re-layouts  3.02 us

commit v1 on v0

v1 whole, which is shorter than its diff:
```python
import functools

import jax
import jax.numpy as jnp
from jax import lax
from jax.experimental import pallas as pl
from jax.experimental.pallas import tpu as pltpu
from jax.sharding import PartitionSpec as P

MOMENTS = 5
HW_MAX = 32
LANES = 128
HALF = LANES // 2
PARTS = 2
ROWS_AT_ONCE = 32
MESH = pl.DeviceIdType.MESH


def split(value):
    parts = []
    for _ in range(PARTS - 1):
        part = value.astype(jnp.bfloat16)
        parts.append(part)
        value = value - part.astype(jnp.float32)
    parts.append(value.astype(jnp.bfloat16))
    return parts


def kernel(
    chans, slabs,
    w_hbm, f_hbm, h_hbm, beam_ref, out_ref,
    w_ref, f_ref, h_ref,
    beams, pieces, band, row_band, sums, passed, crossed, ext, weights, scale,
    small_sem, load_sem, first_send, first_recv, pass_send, pass_recv, cross_send, cross_recv,
    up_send, up_recv, down_send, down_recv, w_send, w_recv,
):
    groups = chans // 2
    me = lax.axis_index("chan")
    slab = lax.axis_index("slab")
    group, core = me // 2, lax.rem(me, 2)
    local_chans, rows, all_cols = beam_ref.shape
    width = all_cols // chans
    chunks = width // LANES
    edge = chunks - 1
    own = groups - 1
    partner = group * 2 + (1 - core)
    not_first, not_last = slab > 0, slab < slabs - 1

    def block_of(slot):
        owner_group = lax.rem(group + slot // 2 + 1, groups)
        return owner_group * 2 + (1 - core if slot % 2 == 0 else core)

    def load(slot, tile):
        col = pl.multiple_of((block_of(slot) * chunks + tile) * LANES, LANES)
        return pltpu.make_async_copy(
            beam_ref.at[:, :, pl.ds(col, LANES)], beams.at[slot, tile], load_sem.at[slot, tile]
        )

    small = [
        pltpu.make_async_copy(source, target, small_sem.at[at])
        for at, (source, target) in enumerate(((h_hbm, h_ref), (w_hbm, w_ref), (f_hbm, f_ref)))
    ]
    for copy in small:
        copy.start()
    for slot in range(chans):
        for tile in range(2):
            load(slot, tile).start()

    @pl.loop(2, chunks)
    def _(tile):
        for slot in range(chans):
            load(slot, tile).start()

    barrier = pltpu.get_barrier_semaphore()
    for offset in range(1, chans):
        pl.semaphore_signal(
            barrier, inc=1, device_id={"chan": lax.rem(me + offset, chans)}, device_id_type=MESH
        )

    @pl.when(not_first)
    def _():
        pl.semaphore_signal(barrier, inc=1, device_id={"slab": slab - 1}, device_id_type=MESH)

    @pl.when(not_last)
    def _():
        pl.semaphore_signal(barrier, inc=1, device_id={"slab": slab + 1}, device_id_type=MESH)

    source = lax.broadcasted_iota(jnp.int32, (2 * LANES, LANES), 0)
    lane = lax.broadcasted_iota(jnp.int32, (2 * LANES, LANES), 1)
    for copy in small:
        copy.wait()

    def put_band(kind, k, near):
        band[kind, k] = jnp.where(near, 1.0, 0.0).astype(jnp.bfloat16)

    target = jnp.where(lane < HALF, lane + LANES, lane)

    @pl.loop(0, MOMENTS)
    def _(k):
        put_band(0, k, jnp.abs(source - target) <= h_ref[k])

    def weight_copy(offset):
        return pltpu.make_async_remote_copy(
            src_ref=weights.at[0], dst_ref=weights.at[offset],
            send_sem=w_send.at[offset - 1], recv_sem=w_recv.at[offset - 1],
            device_id={"chan": lax.rem(me + offset, chans)}, device_id_type=MESH,
        )

    def pass_copy(hop, c):
        return pltpu.make_async_remote_copy(
            src_ref=sums.at[2 * hop, c], dst_ref=passed.at[hop, c],
            send_sem=pass_send.at[hop, c], recv_sem=pass_recv.at[hop, c],
            device_id={"chan": partner}, device_id_type=MESH,
        )

    def first_copy(k):
        return pltpu.make_async_remote_copy(
            src_ref=sums.at[0, 0, k], dst_ref=passed.at[0, 0, k],
            send_sem=first_send.at[k], recv_sem=first_recv.at[k],
            device_id={"chan": partner}, device_id_type=MESH,
        )

    def cross_copy(hop, c, k):
        other = lax.rem(group + hop + 1, groups) * 2 + core
        return pltpu.make_async_remote_copy(
            src_ref=sums.at[2 * hop + 1, c, k], dst_ref=crossed.at[hop, c, k],
            send_sem=cross_send.at[hop, c, k], recv_sem=cross_recv.at[hop, c, k],
            device_id={"chan": other}, device_id_type=MESH,
        )

    def up_copy(c, k):
        return pltpu.make_async_remote_copy(
            src_ref=ext.at[c, k, pl.ds(HW_MAX, HW_MAX)],
            dst_ref=ext.at[c, k, pl.ds(HW_MAX + rows, HW_MAX)],
            send_sem=up_send.at[c, k], recv_sem=up_recv.at[c, k],
            device_id={"slab": slab - 1}, device_id_type=MESH,
        )

    def down_copy(c, k):
        return pltpu.make_async_remote_copy(
            src_ref=ext.at[c, k, pl.ds(rows, HW_MAX)],
            dst_ref=ext.at[c, k, pl.ds(0, HW_MAX)],
            send_sem=down_send.at[c, k], recv_sem=down_recv.at[c, k],
            device_id={"slab": slab + 1}, device_id_type=MESH,
        )

    def moments_of(slot, tile):
        load(slot, tile).wait()
        cols = pl.ds(pl.multiple_of((block_of(slot) * chunks + tile + 1) * LANES, LANES), LANES)

        @pl.loop(0, rows // ROWS_AT_ONCE)
        def _(part):
            first = pl.multiple_of(part * ROWS_AT_ONCE, ROWS_AT_ONCE)
            totals = [None] * MOMENTS
            for chan in range(local_chans):
                weight = w_ref[chan].astype(jnp.float32)
                offset = f_ref[chan]
                term = beams[slot, tile, chan, pl.ds(first, ROWS_AT_ONCE), :] * weight
                for k in range(MOMENTS):
                    if k > 0:
                        term = term * offset
                    totals[k] = term if chan == 0 else totals[k] + term
            for k in range(MOMENTS):
                for at, piece in enumerate(split(totals[k])):
                    pieces[k, pl.ds(first + at * rows, ROWS_AT_ONCE), cols] = piece

    def fold(product):
        result = product[:rows]
        for at in range(1, PARTS):
            result = result + product[at * rows : (at + 1) * rows]
        return result

    def lanes_from(slot, tile):
        first = (block_of(slot) * chunks + tile + 1) * LANES
        return pl.ds(pl.multiple_of(first, LANES), 2 * LANES)

    def columns_of(slot, c, after=None):
        wide = lanes_from(slot, c)
        for k in range(MOMENTS):
            sums[slot, c, k] = fold(
                jnp.dot(pieces[k, :, wide], band[0, k], preferred_element_type=jnp.float32)
            )
            if after is not None:
                after(k)

    def edge_of(slot):
        low, high = lanes_from(slot, -1), lanes_from(slot, chunks - 1)
        for k in range(MOMENTS):
            sums[slot, edge, k] = fold(
                jnp.dot(pieces[k, :, low], band[1, k], preferred_element_type=jnp.float32)
                + jnp.dot(pieces[k, :, high], band[2, k], preferred_element_type=jnp.float32)
            )

    def make(slot, c):
        if isinstance(c, int) and c == edge:
            edge_of(slot)
        else:
            moments_of(slot, c + 1)
            columns_of(slot, c)
        if slot % 2 == 0:
            pass_copy(slot // 2, c).start()

    def send_on(hop, c):
        pass_copy(hop, c).wait_recv()
        for k in range(MOMENTS):
            sums[2 * hop + 1, c, k] = sums[2 * hop + 1, c, k] + passed[hop, c, k]
            cross_copy(hop, c, k).start()

    def finish(c, k):
        value = sums[chans - 1, c, k] + passed[own, c, k]
        for hop in range(own):
            cross_copy(hop, c, k).wait_recv()
            value = value + crossed[hop, c, k]
        ext[c, k, HW_MAX : HW_MAX + rows, :] = value

        @pl.when(not_first)
        def _():
            up_copy(c, k).start()

        @pl.when(not_last)
        def _():
            down_copy(c, k).start()

    left = lax.broadcasted_iota(jnp.int32, (rows, LANES), 1) < HALF

    def rows_of(c, k):
        @pl.when(not_last)
        def _():
            up_copy(c, k).wait_recv()

        @pl.when(not_first)
        def _():
            down_copy(c, k).wait_recv()

        both = jnp.concatenate(split(ext[c, k]), axis=0)
        summed = jnp.dot(row_band[k], both, preferred_element_type=jnp.float32)
        summed = summed * scale[k, 0:1, :]
        if isinstance(c, int) and c == edge:
            at, to = slice(0, LANES), slice(edge * LANES, chunks * LANES)
            out_ref[k, :, at] = jnp.where(left, summed, out_ref[k, :, at])
            out_ref[k, :, to] = jnp.where(left, out_ref[k, :, to], summed)
        else:
            at = pl.ds(pl.multiple_of(c * LANES, LANES), LANES)
            to = pl.ds(pl.multiple_of((c + 1) * LANES, LANES), LANES)
            if isinstance(c, int) and c == 0:
                out_ref[k, :, at] = summed
            else:
                out_ref[k, :, at] = jnp.where(left, out_ref[k, :, at], summed)
            out_ref[k, :, to] = summed

    for slot in range(2):
        moments_of(slot, 0)
        moments_of(slot, 1)
        if slot == 0:
            pl.semaphore_wait(
                barrier, chans - 1 + not_first.astype(jnp.int32) + not_last.astype(jnp.int32)
            )
            columns_of(slot, 0, lambda k: first_copy(k).start())
        else:
            columns_of(slot, 0)
    for k in range(MOMENTS):
        first_copy(k).wait_recv()
        sums[1, 0, k] = sums[1, 0, k] + passed[0, 0, k]
        if own > 0:
            cross_copy(0, 0, k).start()

    total = w_ref[0].astype(jnp.float32)
    for chan in range(1, local_chans):
        total = total + w_ref[chan].astype(jnp.float32)
    weights[0] = jnp.full(weights.shape[1:], total, jnp.float32)
    for offset in range(1, chans):
        weight_copy(offset).start()

    for slot in range(2, chans):
        moments_of(slot, 0)
        make(slot, 0)
    for hop in range(1, own):
        send_on(hop, 0)
    for slot in range(chans):
        make(slot, 1)
    for hop in range(own):
        send_on(hop, 1)
    pass_copy(own, 0).wait_recv()

    @pl.when(slab == 0)
    def _():
        @pl.loop(0, chunks)
        def _(c):
            ext[c, :, 0:HW_MAX, :] = jnp.zeros((MOMENTS, HW_MAX, LANES), jnp.float32)

    @pl.when(slab == slabs - 1)
    def _():
        @pl.loop(0, chunks)
        def _(c):
            ext[c, :, HW_MAX + rows :, :] = jnp.zeros((MOMENTS, HW_MAX, LANES), jnp.float32)

    def set_rest():
        pieces[:, :, 0:LANES] = jnp.zeros(pieces.shape[:2] + (LANES,), jnp.bfloat16)
        pieces[:, :, LANES + all_cols :] = jnp.zeros(pieces.shape[:2] + (LANES,), jnp.bfloat16)
        for offset in range(1, chans):
            weight_copy(offset).wait_recv()
        weight_total = weights[0]
        for offset in range(1, chans):
            weight_total = weight_total + weights[offset]

        @pl.loop(0, MOMENTS)
        def _(k):
            reach = h_ref[k]
            near = jnp.logical_and(lane < HALF, jnp.abs(source - LANES - lane) <= reach)
            put_band(1, k, near)
            near = jnp.logical_and(lane >= HALF, jnp.abs(source - lane) <= reach)
            put_band(2, k, near)
            span = rows + 2 * HW_MAX
            to_row = lax.broadcasted_iota(jnp.int32, (rows, span), 0)
            from_row = lax.broadcasted_iota(jnp.int32, (rows, span), 1)
            near = jnp.abs(from_row - HW_MAX - to_row) <= reach
            near = jnp.where(near, 1.0, 0.0).astype(jnp.bfloat16)
            for part in range(PARTS):
                row_band[k, :, part * span : (part + 1) * span] = near
            divisor = weight_total * (2 * reach + 1).astype(jnp.float32)
            scale[k] = 1.0 / divisor

    def iteration(c, ahead, behind):
        jobs = []
        if ahead is not None:
            for hop in range(own):
                jobs += [functools.partial(make, 2 * hop, ahead)]
                jobs += [functools.partial(make, 2 * hop + 1, ahead)]
            jobs += [functools.partial(make, 2 * own, ahead)]

            def last():
                for hop in range(own):
                    send_on(hop, ahead)
                make(chans - 1, ahead)

            jobs.append(last)
        for k in range(MOMENTS):
            finish(c, k)
            if k < MOMENTS - 1:
                share = -(-len(jobs) // (MOMENTS - 1 - k))
                for job in jobs[:share]:
                    job()
                jobs = jobs[share:]
            if behind is not None:
                rows_of(behind, k)
        if not (isinstance(c, int) and c == edge):
            pass_copy(own, c + 1).wait_recv()

    iteration(0, 2, None)
    set_rest()
    iteration(1, 3, None)
    iteration(2, 4, 0)

    @pl.loop(3, edge - 2)
    def _(c):
        iteration(c, c + 2, c - 2)

    iteration(edge - 2, edge, edge - 4)
    iteration(edge - 1, None, edge - 3)
    iteration(edge, None, edge - 2)

    for k in range(MOMENTS):
        rows_of(edge - 1, k)

    def sent(c):
        for hop in range(groups):
            if not (isinstance(c, int) and c == 0 and hop == 0):
                pass_copy(hop, c).wait_send()
        for k in range(MOMENTS):
            for hop in range(own):
                cross_copy(hop, c, k).wait_send()

            @pl.when(not_first)
            def _():
                up_copy(c, k).wait_send()

            @pl.when(not_last)
            def _():
                down_copy(c, k).wait_send()

    for offset in range(1, chans):
        weight_copy(offset).wait_send()
    for k in range(MOMENTS):
        first_copy(k).wait_send()
    sent(0)

    @pl.loop(1, chunks - 1)
    def _(c):
        sent(c)

    for k in range(MOMENTS):
        rows_of(edge, k)
    sent(edge)


def body(chans, slabs, beam_images, chan_weights, freq_offsets, half_widths):
    local_chans, rows, all_cols = beam_images.shape
    width = all_cols // chans
    chunks, groups = width // LANES, chans // 2
    f32, b16 = jnp.float32, jnp.bfloat16
    dma = pltpu.SemaphoreType.DMA
    hbm = pl.BlockSpec(memory_space=pltpu.HBM)
    small = [
        pltpu.with_memory_space_constraint(value, pltpu.HBM)
        for value in (chan_weights, freq_offsets, half_widths)
    ]
    span = rows + 2 * HW_MAX
    return pl.pallas_call(
        functools.partial(kernel, chans, slabs),
        out_shape=jax.ShapeDtypeStruct((MOMENTS, rows, width), f32),
        in_specs=[hbm, hbm, hbm, hbm],
        out_specs=pl.BlockSpec(memory_space=pltpu.VMEM),
        scratch_shapes=[
            pltpu.SMEM(chan_weights.shape, jnp.int32),
            pltpu.SMEM(freq_offsets.shape, f32),
            pltpu.SMEM(half_widths.shape, jnp.int32),
            pltpu.VMEM((chans, chunks, local_chans, rows, LANES), f32),
            pltpu.VMEM((MOMENTS, PARTS * rows, all_cols + 2 * LANES), b16),
            pltpu.VMEM((3, MOMENTS, 2 * LANES, LANES), b16),
            pltpu.VMEM((MOMENTS, rows, PARTS * span), b16),
            pltpu.VMEM((chans, chunks, MOMENTS, rows, LANES), f32),
            pltpu.VMEM((groups, chunks, MOMENTS, rows, LANES), f32),
            pltpu.VMEM((groups - 1, chunks, MOMENTS, rows, LANES), f32),
            pltpu.VMEM((chunks, MOMENTS, span, LANES), f32),
            pltpu.VMEM((chans, 8, LANES), f32),
            pltpu.VMEM((MOMENTS, 8, LANES), f32),
            dma((3,)),
            dma((chans, chunks)),
            dma((MOMENTS,)),
            dma((MOMENTS,)),
            dma((groups, chunks)),
            dma((groups, chunks)),
            dma((groups - 1, chunks, MOMENTS)),
            dma((groups - 1, chunks, MOMENTS)),
            dma((chunks, MOMENTS)),
            dma((chunks, MOMENTS)),
            dma((chunks, MOMENTS)),
            dma((chunks, MOMENTS)),
            dma((chans - 1,)),
            dma((chans - 1,)),
        ],
        compiler_params=pltpu.CompilerParams(
            collective_id=0, has_side_effects=True, vmem_limit_bytes=44 * 1024 * 1024
        ),
    )(*small, beam_images)


def solution(mesh):
    placed = (P("chan", "slab", None), P("chan"), P("chan"), P())
    return jax.shard_map(
        functools.partial(body, mesh.shape["chan"], mesh.shape["slab"]),
        mesh=mesh, in_specs=placed, out_specs=P(None, "slab", "chan"), check_vma=False,
    )
```

time: 48.5 us -> 42.8 us (0.88)
  the two profiles are of different devices: /device:TPU:9 before, /device:TPU:0 now
where the time goes in v1:
time: 42.8 us; the launch traced here: 42.7 us
  Pallas kernels  41.6 us (97%)
  local copies, waits for them, and re-layouts  1.06 us (2%)
    pallas_call x1, Pallas kernels, body(): pl.pallas_call(functools.partial(kernel, chans, slabs), out_shape=jax.Sha...  41.6 us
    unnamed x1, local copies, waits for them, and re-layouts  1.06 us

profile of v1, /device:TPU:0, one launch (start us, length us, event | category | flops | bytes accessed | tf_op | source)
XLA Modules:
  0.0 42.7 jit_solution(16468278747136097516)
XLA Ops:
  0.0 41.6 %shard_map.46 = f32[5,64,1024]{2,1,0:T(8,128)S(1)} custom-call(s32[16]{0:T(128)} %w_hbm.1, f32[16]{0:T(128)} %f_hbm.1, s32[5]{0:T(128)} %h_hbm.1, f32[16,64,4096]{2,1,0:T(8,128)} %beam_ref.1), custom_call_target="tpu_custom_call" | custom-call | tf_op jit(solution)/shard_map/pallas_call | solution.py:408
  41.6 1.1 %copy.6 = f32[5,64,1024]{2,1,0:T(8,128)} copy(f32[5,64,1024]{2,1,0:T(8,128)S(1)} %shard_map.46) | data formatting | bytes 2621440

commit v2 on v1

--- a/solution.py
+++ b/solution.py
@@ -13,6 +13,10 @@
 HALF = LANES // 2
 PARTS = 2
 ROWS_AT_ONCE = 32
+FIRST = 2
+PASS_TURNS = 3
+CROSS_TURNS = 4
+ROW_TURNS = 5
 MESH = pl.DeviceIdType.MESH
 
 
@@ -31,7 +35,7 @@
     w_hbm, f_hbm, h_hbm, beam_ref, out_ref,
     w_ref, f_ref, h_ref,
     beams, pieces, band, row_band, sums, passed, crossed, ext, weights, scale,
-    small_sem, load_sem, first_send, first_recv, pass_send, pass_recv, cross_send, cross_recv,
+    small_sem, first_sem, load_sem, pass_send, pass_recv, cross_send, cross_recv,
     up_send, up_recv, down_send, down_recv, w_send, w_recv,
 ):
     groups = chans // 2
@@ -52,9 +56,13 @@
 
     def load(slot, tile):
         col = pl.multiple_of((block_of(slot) * chunks + tile) * LANES, LANES)
+        sem = first_sem.at[slot] if isinstance(tile, int) else load_sem.at[tile - FIRST]
         return pltpu.make_async_copy(
-            beam_ref.at[:, :, pl.ds(col, LANES)], beams.at[slot, tile], load_sem.at[slot, tile]
-        )
+            beam_ref.at[:, :, pl.ds(col, LANES)], beams.at[tile, slot], sem
+        )
+
+    def drain(ref, sem):
+        pltpu.make_async_copy(ref, ref, sem).wait()
 
     small = [
         pltpu.make_async_copy(source, target, small_sem.at[at])
@@ -63,10 +71,10 @@
     for copy in small:
         copy.start()
     for slot in range(chans):
-        for tile in range(2):
+        for tile in range(FIRST):
             load(slot, tile).start()
 
-    @pl.loop(2, chunks)
+    @pl.loop(FIRST, chunks)
     def _(tile):
         for slot in range(chans):
             load(slot, tile).start()
@@ -102,21 +110,14 @@
     def weight_copy(offset):
         return pltpu.make_async_remote_copy(
             src_ref=weights.at[0], dst_ref=weights.at[offset],
-            send_sem=w_send.at[offset - 1], recv_sem=w_recv.at[offset - 1],
+            send_sem=w_send.at[0], recv_sem=w_recv.at[offset - 1],
             device_id={"chan": lax.rem(me + offset, chans)}, device_id_type=MESH,
         )
 
     def pass_copy(hop, c):
         return pltpu.make_async_remote_copy(
             src_ref=sums.at[2 * hop, c], dst_ref=passed.at[hop, c],
-            send_sem=pass_send.at[hop, c], recv_sem=pass_recv.at[hop, c],
-            device_id={"chan": partner}, device_id_type=MESH,
-        )
-
-    def first_copy(k):
-        return pltpu.make_async_remote_copy(
-            src_ref=sums.at[0, 0, k], dst_ref=passed.at[0, 0, k],
-            send_sem=first_send.at[k], recv_sem=first_recv.at[k],
+            send_sem=pass_send.at[hop], recv_sem=pass_recv.at[hop, lax.rem(c, PASS_TURNS)],
             device_id={"chan": partner}, device_id_type=MESH,
         )
 
@@ -124,7 +125,8 @@
         other = lax.rem(group + hop + 1, groups) * 2 + core
         return pltpu.make_async_remote_copy(
             src_ref=sums.at[2 * hop + 1, c, k], dst_ref=crossed.at[hop, c, k],
-            send_sem=cross_send.at[hop, c, k], recv_sem=cross_recv.at[hop, c, k],
+            send_sem=cross_send.at[hop],
+            recv_sem=cross_recv.at[hop, lax.rem(c, CROSS_TURNS), k],
             device_id={"chan": other}, device_id_type=MESH,
         )
 
@@ -132,7 +134,7 @@
         return pltpu.make_async_remote_copy(
             src_ref=ext.at[c, k, pl.ds(HW_MAX, HW_MAX)],
             dst_ref=ext.at[c, k, pl.ds(HW_MAX + rows, HW_MAX)],
-            send_sem=up_send.at[c, k], recv_sem=up_recv.at[c, k],
+            send_sem=up_send.at[0], recv_sem=up_recv.at[lax.rem(c, ROW_TURNS), k],
             device_id={"slab": slab - 1}, device_id_type=MESH,
         )
 
@@ -140,12 +142,11 @@
         return pltpu.make_async_remote_copy(
             src_ref=ext.at[c, k, pl.ds(rows, HW_MAX)],
             dst_ref=ext.at[c, k, pl.ds(0, HW_MAX)],
-            send_sem=down_send.at[c, k], recv_sem=down_recv.at[c, k],
+            send_sem=down_send.at[0], recv_sem=down_recv.at[lax.rem(c, ROW_TURNS), k],
             device_id={"slab": slab + 1}, device_id_type=MESH,
         )
 
     def moments_of(slot, tile):
-        load(slot, tile).wait()
         cols = pl.ds(pl.multiple_of((block_of(slot) * chunks + tile + 1) * LANES, LANES), LANES)
 
         @pl.loop(0, rows // ROWS_AT_ONCE)
@@ -155,7 +156,7 @@
             for chan in range(local_chans):
                 weight = w_ref[chan].astype(jnp.float32)
                 offset = f_ref[chan]
-                term = beams[slot, tile, chan, pl.ds(first, ROWS_AT_ONCE), :] * weight
+                term = beams[tile, slot, chan, pl.ds(first, ROWS_AT_ONCE), :] * weight
                 for k in range(MOMENTS):
                     if k > 0:
                         term = term * offset
@@ -174,14 +175,12 @@
         first = (block_of(slot) * chunks + tile + 1) * LANES
         return pl.ds(pl.multiple_of(first, LANES), 2 * LANES)
 
-    def columns_of(slot, c, after=None):
+    def columns_of(slot, c):
         wide = lanes_from(slot, c)
         for k in range(MOMENTS):
             sums[slot, c, k] = fold(
                 jnp.dot(pieces[k, :, wide], band[0, k], preferred_element_type=jnp.float32)
             )
-            if after is not None:
-                after(k)
 
     def edge_of(slot):
         low, high = lanes_from(slot, -1), lanes_from(slot, chunks - 1)
@@ -248,21 +247,23 @@
                 out_ref[k, :, at] = jnp.where(left, out_ref[k, :, at], summed)
             out_ref[k, :, to] = summed
 
-    for slot in range(2):
-        moments_of(slot, 0)
-        moments_of(slot, 1)
-        if slot == 0:
-            pl.semaphore_wait(
-                barrier, chans - 1 + not_first.astype(jnp.int32) + not_last.astype(jnp.int32)
-            )
-            columns_of(slot, 0, lambda k: first_copy(k).start())
-        else:
-            columns_of(slot, 0)
-    for k in range(MOMENTS):
-        first_copy(k).wait_recv()
-        sums[1, 0, k] = sums[1, 0, k] + passed[0, 0, k]
-        if own > 0:
-            cross_copy(0, 0, k).start()
+    def start(slot):
+        drain(beams.at[0:FIRST, slot], first_sem.at[slot])
+        for tile in range(FIRST - 1):
+            moments_of(slot, tile)
+        make(slot, 0)
+
+    drain(beams.at[0:FIRST, 0], first_sem.at[0])
+    for tile in range(FIRST):
+        moments_of(0, tile)
+    columns_of(0, 0)
+    pl.semaphore_wait(
+        barrier, chans - 1 + not_first.astype(jnp.int32) + not_last.astype(jnp.int32)
+    )
+    pass_copy(0, 0).start()
+    start(1)
+    if own > 0:
+        send_on(0, 0)
 
     total = w_ref[0].astype(jnp.float32)
     for chan in range(1, local_chans):
@@ -272,10 +273,10 @@
         weight_copy(offset).start()
 
     for slot in range(2, chans):
-        moments_of(slot, 0)
-        make(slot, 0)
+        start(slot)
     for hop in range(1, own):
         send_on(hop, 0)
+    drain(beams.at[FIRST], load_sem.at[0])
     for slot in range(chans):
         make(slot, 1)
     for hop in range(own):
@@ -323,17 +324,9 @@
     def iteration(c, ahead, behind):
         jobs = []
         if ahead is not None:
-            for hop in range(own):
-                jobs += [functools.partial(make, 2 * hop, ahead)]
-                jobs += [functools.partial(make, 2 * hop + 1, ahead)]
-            jobs += [functools.partial(make, 2 * own, ahead)]
-
-            def last():
-                for hop in range(own):
-                    send_on(hop, ahead)
-                make(chans - 1, ahead)
-
-            jobs.append(last)
+            jobs = [functools.partial(make, slot, ahead) for slot in range(chans)]
+            if not (isinstance(ahead, int) and ahead == edge):
+                drain(beams.at[ahead + 1], load_sem.at[ahead + 1 - FIRST])
         for k in range(MOMENTS):
             finish(c, k)
             if k < MOMENTS - 1:
@@ -341,6 +334,9 @@
                 for job in jobs[:share]:
                     job()
                 jobs = jobs[share:]
+            elif ahead is not None:
+                for hop in range(own):
+                    send_on(hop, ahead)
             if behind is not None:
                 rows_of(behind, k)
         if not (isinstance(c, int) and c == edge):
@@ -362,35 +358,22 @@
     for k in range(MOMENTS):
         rows_of(edge - 1, k)
 
-    def sent(c):
-        for hop in range(groups):
-            if not (isinstance(c, int) and c == 0 and hop == 0):
-                pass_copy(hop, c).wait_send()
-        for k in range(MOMENTS):
-            for hop in range(own):
-                cross_copy(hop, c, k).wait_send()
-
-            @pl.when(not_first)
-            def _():
-                up_copy(c, k).wait_send()
-
-            @pl.when(not_last)
-            def _():
-                down_copy(c, k).wait_send()
-
-    for offset in range(1, chans):
-        weight_copy(offset).wait_send()
-    for k in range(MOMENTS):
-        first_copy(k).wait_send()
-    sent(0)
-
-    @pl.loop(1, chunks - 1)
-    def _(c):
-        sent(c)
-
     for k in range(MOMENTS):
         rows_of(edge, k)
-    sent(edge)
+
+    drain(weights.at[1:chans], w_send.at[0])
+    for hop in range(groups):
+        drain(sums.at[2 * hop], pass_send.at[hop])
+    for hop in range(own):
+        drain(sums.at[2 * hop + 1], cross_send.at[hop])
+
+    @pl.when(not_first)
+    def _():
+        drain(ext.at[:, :, HW_MAX : 2 * HW_MAX], up_send.at[0])
+
+    @pl.when(not_last)
+    def _():
+        drain(ext.at[:, :, rows : rows + HW_MAX], down_send.at[0])
 
 
 def body(chans, slabs, beam_images, chan_weights, freq_offsets, half_widths):
@@ -414,7 +397,7 @@
             pltpu.SMEM(chan_weights.shape, jnp.int32),
             pltpu.SMEM(freq_offsets.shape, f32),
             pltpu.SMEM(half_widths.shape, jnp.int32),
-            pltpu.VMEM((chans, chunks, local_chans, rows, LANES), f32),
+            pltpu.VMEM((chunks, chans, local_chans, rows, LANES), f32),
             pltpu.VMEM((MOMENTS, PARTS * rows, all_cols + 2 * LANES), b16),
             pltpu.VMEM((3, MOMENTS, 2 * LANES, LANES), b16),
             pltpu.VMEM((MOMENTS, rows, PARTS * span), b16),
@@ -425,18 +408,17 @@
             pltpu.VMEM((chans, 8, LANES), f32),
             pltpu.VMEM((MOMENTS, 8, LANES), f32),
             dma((3,)),
-            dma((chans, chunks)),
-            dma((MOMENTS,)),
-            dma((MOMENTS,)),
-            dma((groups, chunks)),
-            dma((groups, chunks)),
-            dma((groups - 1, chunks, MOMENTS)),
-            dma((groups - 1, chunks, MOMENTS)),
-            dma((chunks, MOMENTS)),
-            dma((chunks, MOMENTS)),
-            dma((chunks, MOMENTS)),
-            dma((chunks, MOMENTS)),
-            dma((chans - 1,)),
+            dma((chans,)),
+            dma((chunks - FIRST,)),
+            dma((groups,)),
+            dma((groups, PASS_TURNS)),
+            dma((groups - 1,)),
+            dma((groups - 1, CROSS_TURNS, MOMENTS)),
+            dma((1,)),
+            dma((ROW_TURNS, MOMENTS)),
+            dma((1,)),
+            dma((ROW_TURNS, MOMENTS)),
+            dma((1,)),
             dma((chans - 1,)),
         ],
         compiler_params=pltpu.CompilerParams(

time: 42.8 us -> 40.8 us (0.953)
  Pallas kernels: 41.6 us -> 39.6 us
    pallas_call x1, Pallas kernels: 41.6 us -> 39.6 us  [body(): pl.pallas_call(functools.partial(kernel, chans, slabs), out_shape=jax.Sha...]
where the time goes in v2:
time: 40.8 us; the launch traced here: 40.7 us
  Pallas kernels  39.6 us (97%)
  local copies, waits for them, and re-layouts  1.06 us (3%)
    pallas_call x1, Pallas kernels, body(): pl.pallas_call(functools.partial(kernel, chans, slabs), out_shape=jax.Sha...  39.6 us
    unnamed x1, local copies, waits for them, and re-layouts  1.06 us

profile of v2, /device:TPU:0, one launch (start us, length us, event | category | flops | bytes accessed | tf_op | source)
XLA Modules:
  0.0 40.7 jit_solution(1779930394537907462)
XLA Ops:
  0.0 39.6 %shard_map.46 = f32[5,64,1024]{2,1,0:T(8,128)S(1)} custom-call(s32[16]{0:T(128)} %w_hbm.1, f32[16]{0:T(128)} %f_hbm.1, s32[5]{0:T(128)} %h_hbm.1, f32[16,64,4096]{2,1,0:T(8,128)} %beam_ref.1), custom_call_target="tpu_custom_call" | custom-call | tf_op jit(solution)/shard_map/pallas_call | solution.py:391
  39.6 1.1 %copy.6 = f32[5,64,1024]{2,1,0:T(8,128)} copy(f32[5,64,1024]{2,1,0:T(8,128)S(1)} %shard_map.46) | data formatting | bytes 2621440

commit v3 on v2

--- a/solution.py
+++ b/solution.py
@@ -30,7 +30,29 @@
     return parts
 
 
-def kernel(
+def kernel(chans, slabs, *refs):
+    chunks = refs[3].shape[2] // chans // LANES
+    groups = chans // 2
+    dma = pltpu.SemaphoreType.DMA
+    pl.run_scoped(
+        functools.partial(scoped, chans, slabs, *refs),
+        dma((3,)),
+        dma((chans, FIRST)),
+        dma((chunks - FIRST,)),
+        dma((groups,)),
+        dma((groups, PASS_TURNS)),
+        dma((groups - 1,)),
+        dma((groups - 1, CROSS_TURNS, MOMENTS)),
+        dma((1,)),
+        dma((ROW_TURNS, MOMENTS)),
+        dma((1,)),
+        dma((ROW_TURNS, MOMENTS)),
+        dma((1,)),
+        dma((chans - 1,)),
+    )
+
+
+def scoped(
     chans, slabs,
     w_hbm, f_hbm, h_hbm, beam_ref, out_ref,
     w_ref, f_ref, h_ref,
@@ -56,7 +78,7 @@
 
     def load(slot, tile):
         col = pl.multiple_of((block_of(slot) * chunks + tile) * LANES, LANES)
-        sem = first_sem.at[slot] if isinstance(tile, int) else load_sem.at[tile - FIRST]
+        sem = first_sem.at[slot, tile] if isinstance(tile, int) else load_sem.at[tile - FIRST]
         return pltpu.make_async_copy(
             beam_ref.at[:, :, pl.ds(col, LANES)], beams.at[tile, slot], sem
         )
@@ -248,15 +270,12 @@
             out_ref[k, :, to] = summed
 
     def start(slot):
-        drain(beams.at[0:FIRST, slot], first_sem.at[slot])
-        for tile in range(FIRST - 1):
+        for tile in range(FIRST):
+            load(slot, tile).wait()
             moments_of(slot, tile)
-        make(slot, 0)
-
-    drain(beams.at[0:FIRST, 0], first_sem.at[0])
-    for tile in range(FIRST):
-        moments_of(0, tile)
-    columns_of(0, 0)
+        columns_of(slot, 0)
+
+    start(0)
     pl.semaphore_wait(
         barrier, chans - 1 + not_first.astype(jnp.int32) + not_last.astype(jnp.int32)
     )
@@ -274,6 +293,8 @@
 
     for slot in range(2, chans):
         start(slot)
+        if slot % 2 == 0:
+            pass_copy(slot // 2, 0).start()
     for hop in range(1, own):
         send_on(hop, 0)
     drain(beams.at[FIRST], load_sem.at[0])
@@ -381,7 +402,6 @@
     width = all_cols // chans
     chunks, groups = width // LANES, chans // 2
     f32, b16 = jnp.float32, jnp.bfloat16
-    dma = pltpu.SemaphoreType.DMA
     hbm = pl.BlockSpec(memory_space=pltpu.HBM)
     small = [
         pltpu.with_memory_space_constraint(value, pltpu.HBM)
@@ -407,19 +427,6 @@
             pltpu.VMEM((chunks, MOMENTS, span, LANES), f32),
             pltpu.VMEM((chans, 8, LANES), f32),
             pltpu.VMEM((MOMENTS, 8, LANES), f32),
-            dma((3,)),
-            dma((chans,)),
-            dma((chunks - FIRST,)),
-            dma((groups,)),
-            dma((groups, PASS_TURNS)),
-            dma((groups - 1,)),
-            dma((groups - 1, CROSS_TURNS, MOMENTS)),
-            dma((1,)),
-            dma((ROW_TURNS, MOMENTS)),
-            dma((1,)),
-            dma((ROW_TURNS, MOMENTS)),
-            dma((1,)),
-            dma((chans - 1,)),
         ],
         compiler_params=pltpu.CompilerParams(
             collective_id=0, has_side_effects=True, vmem_limit_bytes=44 * 1024 * 1024

time: 40.8 us -> 39.8 us (0.975)
  Pallas kernels: 39.6 us -> 38.6 us
    pallas_call x1, Pallas kernels: 39.6 us -> 38.6 us  [body(): pl.pallas_call(functools.partial(kernel, chans, slabs), out_shape=jax.Sha...]
where the time goes in v3:
time: 39.8 us; the launch traced here: 39.6 us
  Pallas kernels  38.6 us (97%)
  local copies, waits for them, and re-layouts  1.06 us (3%)
    pallas_call x1, Pallas kernels, body(): pl.pallas_call(functools.partial(kernel, chans, slabs), out_shape=jax.Sha...  38.6 us
    unnamed x1, local copies, waits for them, and re-layouts  1.06 us

profile of v3, /device:TPU:0, one launch (start us, length us, event | category | flops | bytes accessed | tf_op | source)
XLA Modules:
  0.0 39.6 jit_solution(18174262927761408781)
XLA Ops:
  0.0 38.6 %shard_map.46 = f32[5,64,1024]{2,1,0:T(8,128)S(1)} custom-call(s32[16]{0:T(128)} %refs_0_.1, f32[16]{0:T(128)} %refs_1_.1, s32[5]{0:T(128)} %refs_2_.1, f32[16,64,4096]{2,1,0:T(8,128)} %refs_3_.1), custom_call_target="tpu_custom_call" | custom-call | tf_op jit(solution)/shard_map/pallas_call | solution.py:411
  38.6 1.1 %copy.6 = f32[5,64,1024]{2,1,0:T(8,128)} copy(f32[5,64,1024]{2,1,0:T(8,128)S(1)} %shard_map.46) | data formatting | bytes 2621440

commit v4 on v3

--- a/solution.py
+++ b/solution.py
@@ -14,9 +14,9 @@
 PARTS = 2
 ROWS_AT_ONCE = 32
 FIRST = 2
-PASS_TURNS = 3
-CROSS_TURNS = 4
-ROW_TURNS = 5
+LATE = 2
+LATE_AT = 3
+HALVES = 2
 MESH = pl.DeviceIdType.MESH
 
 
@@ -40,13 +40,13 @@
         dma((chans, FIRST)),
         dma((chunks - FIRST,)),
         dma((groups,)),
-        dma((groups, PASS_TURNS)),
+        dma((groups, chunks)),
         dma((groups - 1,)),
-        dma((groups - 1, CROSS_TURNS, MOMENTS)),
+        dma((groups - 1, chunks, MOMENTS, HALVES)),
         dma((1,)),
-        dma((ROW_TURNS, MOMENTS)),
+        dma((chunks * MOMENTS + (groups - 1) * LATE,)),
         dma((1,)),
-        dma((ROW_TURNS, MOMENTS)),
+        dma((chunks * MOMENTS + (groups - 1) * LATE,)),
         dma((1,)),
         dma((chans - 1,)),
     )
@@ -56,7 +56,7 @@
     chans, slabs,
     w_hbm, f_hbm, h_hbm, beam_ref, out_ref,
     w_ref, f_ref, h_ref,
-    beams, pieces, band, row_band, sums, passed, crossed, ext, weights, scale,
+    beams, pieces, band, row_band, sums, passed, crossed, ext, late, weights, scale,
     small_sem, first_sem, load_sem, pass_send, pass_recv, cross_send, cross_recv,
     up_send, up_recv, down_send, down_recv, w_send, w_recv,
 ):
@@ -86,6 +86,20 @@
     def drain(ref, sem):
         pltpu.make_async_copy(ref, ref, sem).wait()
 
+    barrier = pltpu.get_barrier_semaphore()
+    for offset in range(1, chans):
+        pl.semaphore_signal(
+            barrier, inc=1, device_id={"chan": lax.rem(me + offset, chans)}, device_id_type=MESH
+        )
+
+    @pl.when(not_first)
+    def _():
+        pl.semaphore_signal(barrier, inc=1, device_id={"slab": slab - 1}, device_id_type=MESH)
+
+    @pl.when(not_last)
+    def _():
+        pl.semaphore_signal(barrier, inc=1, device_id={"slab": slab + 1}, device_id_type=MESH)
+
     small = [
         pltpu.make_async_copy(source, target, small_sem.at[at])
         for at, (source, target) in enumerate(((h_hbm, h_ref), (w_hbm, w_ref), (f_hbm, f_ref)))
@@ -101,20 +115,6 @@
         for slot in range(chans):
             load(slot, tile).start()
 
-    barrier = pltpu.get_barrier_semaphore()
-    for offset in range(1, chans):
-        pl.semaphore_signal(
-            barrier, inc=1, device_id={"chan": lax.rem(me + offset, chans)}, device_id_type=MESH
-        )
-
-    @pl.when(not_first)
-    def _():
-        pl.semaphore_signal(barrier, inc=1, device_id={"slab": slab - 1}, device_id_type=MESH)
-
-    @pl.when(not_last)
-    def _():
-        pl.semaphore_signal(barrier, inc=1, device_id={"slab": slab + 1}, device_id_type=MESH)
-
     source = lax.broadcasted_iota(jnp.int32, (2 * LANES, LANES), 0)
     lane = lax.broadcasted_iota(jnp.int32, (2 * LANES, LANES), 1)
     for copy in small:
@@ -139,41 +139,56 @@
     def pass_copy(hop, c):
         return pltpu.make_async_remote_copy(
             src_ref=sums.at[2 * hop, c], dst_ref=passed.at[hop, c],
-            send_sem=pass_send.at[hop], recv_sem=pass_recv.at[hop, lax.rem(c, PASS_TURNS)],
+            send_sem=pass_send.at[hop], recv_sem=pass_recv.at[hop, c],
             device_id={"chan": partner}, device_id_type=MESH,
         )
 
-    def cross_copy(hop, c, k):
-        other = lax.rem(group + hop + 1, groups) * 2 + core
+    def other(hop):
+        return lax.rem(group + hop + 1, groups) * 2 + core
+
+    def cross_copy(hop, c, k, half):
+        part = pl.ds(half * rows // HALVES, rows // HALVES)
         return pltpu.make_async_remote_copy(
-            src_ref=sums.at[2 * hop + 1, c, k], dst_ref=crossed.at[hop, c, k],
-            send_sem=cross_send.at[hop],
-            recv_sem=cross_recv.at[hop, lax.rem(c, CROSS_TURNS), k],
-            device_id={"chan": other}, device_id_type=MESH,
-        )
-
-    def up_copy(c, k):
+            src_ref=sums.at[2 * hop + 1, c, k, part], dst_ref=crossed.at[hop, c, k, part],
+            send_sem=cross_send.at[hop], recv_sem=cross_recv.at[hop, c, k, half],
+            device_id={"chan": other(hop)}, device_id_type=MESH,
+        )
+
+    def late_copy(hop, j):
         return pltpu.make_async_remote_copy(
-            src_ref=ext.at[c, k, pl.ds(HW_MAX, HW_MAX)],
-            dst_ref=ext.at[c, k, pl.ds(HW_MAX + rows, HW_MAX)],
-            send_sem=up_send.at[0], recv_sem=up_recv.at[lax.rem(c, ROW_TURNS), k],
+            src_ref=late.at[hop, j], dst_ref=crossed.at[hop, 0, MOMENTS - LATE + j],
+            send_sem=cross_send.at[hop], recv_sem=cross_recv.at[hop, 0, MOMENTS - LATE + j, 0],
+            device_id={"chan": other(hop)}, device_id_type=MESH,
+        )
+
+    def place(c, k):
+        return c * MOMENTS + k
+
+    def late_place(hop, j):
+        if hop == own:
+            return place(0, MOMENTS - LATE + j)
+        return chunks * MOMENTS + hop * LATE + j
+
+    def up_copy(at):
+        return pltpu.make_async_remote_copy(
+            src_ref=ext.at[at, pl.ds(HW_MAX, HW_MAX)],
+            dst_ref=ext.at[at, pl.ds(HW_MAX + rows, HW_MAX)],
+            send_sem=up_send.at[0], recv_sem=up_recv.at[at],
             device_id={"slab": slab - 1}, device_id_type=MESH,
         )
 
-    def down_copy(c, k):
+    def down_copy(at):
         return pltpu.make_async_remote_copy(
-            src_ref=ext.at[c, k, pl.ds(rows, HW_MAX)],
-            dst_ref=ext.at[c, k, pl.ds(0, HW_MAX)],
-            send_sem=down_send.at[0], recv_sem=down_recv.at[lax.rem(c, ROW_TURNS), k],
+            src_ref=ext.at[at, pl.ds(rows, HW_MAX)],
+            dst_ref=ext.at[at, pl.ds(0, HW_MAX)],
+            send_sem=down_send.at[0], recv_sem=down_recv.at[at],
             device_id={"slab": slab + 1}, device_id_type=MESH,
         )
 
     def moments_of(slot, tile):
         cols = pl.ds(pl.multiple_of((block_of(slot) * chunks + tile + 1) * LANES, LANES), LANES)
 
-        @pl.loop(0, rows // ROWS_AT_ONCE)
-        def _(part):
-            first = pl.multiple_of(part * ROWS_AT_ONCE, ROWS_AT_ONCE)
+        for first in range(0, rows, ROWS_AT_ONCE):
             totals = [None] * MOMENTS
             for chan in range(local_chans):
                 weight = w_ref[chan].astype(jnp.float32)
@@ -212,50 +227,93 @@
                 + jnp.dot(pieces[k, :, high], band[2, k], preferred_element_type=jnp.float32)
             )
 
-    def make(slot, c):
+    def make(slot, c, following=()):
         if isinstance(c, int) and c == edge:
             edge_of(slot)
         else:
-            moments_of(slot, c + 1)
             columns_of(slot, c)
+        for other_slot, tile in following:
+            moments_of(other_slot, tile)
         if slot % 2 == 0:
             pass_copy(slot // 2, c).start()
+
+    def makes(c):
+        jobs = []
+        for slot in range(chans):
+            if isinstance(c, int) and c == edge:
+                following = ()
+            elif slot < chans - 1:
+                following = ((slot + 1, c + 1),)
+            elif isinstance(c, int) and c == edge - 1:
+                following = ()
+            else:
+                following = ((0, c + 2),)
+            jobs.append(functools.partial(make, slot, c, following))
+        return jobs
+
+    def crosses(c, k):
+        return not (isinstance(c, int) and c == 0 and k >= MOMENTS - LATE)
 
     def send_on(hop, c):
         pass_copy(hop, c).wait_recv()
         for k in range(MOMENTS):
-            sums[2 * hop + 1, c, k] = sums[2 * hop + 1, c, k] + passed[hop, c, k]
-            cross_copy(hop, c, k).start()
-
-    def finish(c, k):
-        value = sums[chans - 1, c, k] + passed[own, c, k]
-        for hop in range(own):
-            cross_copy(hop, c, k).wait_recv()
-            value = value + crossed[hop, c, k]
-        ext[c, k, HW_MAX : HW_MAX + rows, :] = value
-
+            value = sums[2 * hop + 1, c, k] + passed[hop, c, k]
+            if crosses(c, k):
+                sums[2 * hop + 1, c, k] = value
+                for half in range(HALVES):
+                    cross_copy(hop, c, k, half).start()
+            else:
+                share(late_place(hop, k - MOMENTS + LATE), value)
+
+    def send_up(at):
         @pl.when(not_first)
         def _():
-            up_copy(c, k).start()
-
+            up_copy(at).start()
+
+    def send_down(at):
         @pl.when(not_last)
         def _():
-            down_copy(c, k).start()
+            down_copy(at).start()
+
+    def share(at, value):
+        ext[at, HW_MAX : HW_MAX + rows, :] = value
+        send_up(at)
+        send_down(at)
+
+    def finish(c, k):
+        at = place(c, k)
+        for half in range(HALVES):
+            first, count = half * rows // HALVES, rows // HALVES
+            part = slice(first, first + count)
+            value = sums[chans - 1, c, k, part] + passed[own, c, k, part]
+            for hop in range(own):
+                cross_copy(hop, c, k, half).wait_recv()
+                value = value + crossed[hop, c, k, part]
+            ext[at, HW_MAX + first : HW_MAX + first + count, :] = value
+            if half == 0 and HALVES == 2:
+                send_up(at)
+        if HALVES == 1:
+            send_up(at)
+        send_down(at)
 
     left = lax.broadcasted_iota(jnp.int32, (rows, LANES), 1) < HALF
 
-    def rows_of(c, k):
+    def row_sums(at, k):
         @pl.when(not_last)
         def _():
-            up_copy(c, k).wait_recv()
+            up_copy(at).wait_recv()
 
         @pl.when(not_first)
         def _():
-            down_copy(c, k).wait_recv()
-
-        both = jnp.concatenate(split(ext[c, k]), axis=0)
-        summed = jnp.dot(row_band[k], both, preferred_element_type=jnp.float32)
-        summed = summed * scale[k, 0:1, :]
+            down_copy(at).wait_recv()
+
+        both = jnp.concatenate(split(ext[at]), axis=0)
+        return jnp.dot(row_band[k], both, preferred_element_type=jnp.float32)
+
+    def rows_of(c, k):
+        if not crosses(c, k):
+            return
+        summed = row_sums(place(c, k), k) * scale[k, 0:1, :]
         if isinstance(c, int) and c == edge:
             at, to = slice(0, LANES), slice(edge * LANES, chunks * LANES)
             out_ref[k, :, at] = jnp.where(left, summed, out_ref[k, :, at])
@@ -269,20 +327,53 @@
                 out_ref[k, :, at] = jnp.where(left, out_ref[k, :, at], summed)
             out_ref[k, :, to] = summed
 
-    def start(slot):
-        for tile in range(FIRST):
-            load(slot, tile).wait()
-            moments_of(slot, tile)
-        columns_of(slot, 0)
-
-    start(0)
+    def late_rows(hop):
+        for j in range(LATE):
+            late[hop, j] = row_sums(late_place(hop, j), MOMENTS - LATE + j)
+
+    def late_out(j):
+        k = MOMENTS - LATE + j
+        summed = late[own, j]
+        for hop in range(own):
+            late_copy(hop, j).wait_recv()
+            summed = summed + crossed[hop, 0, k]
+        summed = summed * scale[k, 0:1, :]
+        out_ref[k, :, 0:LANES] = summed
+        out_ref[k, :, LANES : 2 * LANES] = jnp.where(
+            left, summed, out_ref[k, :, LANES : 2 * LANES]
+        )
+
+    @pl.when(slab == 0)
+    def _():
+        @pl.loop(0, ext.shape[0])
+        def _(at):
+            ext[at, 0:HW_MAX, :] = jnp.zeros((HW_MAX, LANES), jnp.float32)
+
+    @pl.when(slab == slabs - 1)
+    def _():
+        @pl.loop(0, ext.shape[0])
+        def _(at):
+            ext[at, HW_MAX + rows :, :] = jnp.zeros((HW_MAX, LANES), jnp.float32)
+
+    for tile in range(FIRST):
+        load(0, tile).wait()
+        moments_of(0, tile)
+    columns_of(0, 0)
     pl.semaphore_wait(
         barrier, chans - 1 + not_first.astype(jnp.int32) + not_last.astype(jnp.int32)
     )
     pass_copy(0, 0).start()
-    start(1)
-    if own > 0:
-        send_on(0, 0)
+    for slot in range(1, 2 * own):
+        for tile in range(FIRST):
+            load(slot, tile).wait()
+            if slot % 2 == 1 or tile > 0:
+                moments_of(slot, tile)
+        if slot % 2 == 1:
+            load(slot + 1, 0).wait()
+            make(slot, 0, ((slot + 1, 0),))
+            send_on(slot // 2, 0)
+        else:
+            make(slot, 0)
 
     total = w_ref[0].astype(jnp.float32)
     for chan in range(1, local_chans):
@@ -291,32 +382,27 @@
     for offset in range(1, chans):
         weight_copy(offset).start()
 
-    for slot in range(2, chans):
-        start(slot)
-        if slot % 2 == 0:
-            pass_copy(slot // 2, 0).start()
-    for hop in range(1, own):
-        send_on(hop, 0)
+    load(2 * own, 1).wait()
+    moments_of(2 * own, 1)
+    for tile in range(FIRST):
+        load(chans - 1, tile).wait()
+    make(2 * own, 0, tuple((chans - 1, tile) for tile in range(FIRST)))
     drain(beams.at[FIRST], load_sem.at[0])
-    for slot in range(chans):
-        make(slot, 1)
+    make(chans - 1, 0, ((0, FIRST),))
+    jobs = makes(1)
+    for job in jobs[:-1]:
+        job()
+    pass_copy(own, 0).wait_recv()
+    for j in range(LATE):
+        k = MOMENTS - LATE + j
+        share(late_place(own, j), sums[chans - 1, 0, k] + passed[own, 0, k])
+    drain(beams.at[FIRST + 1], load_sem.at[1])
+    jobs[-1]()
     for hop in range(own):
         send_on(hop, 1)
-    pass_copy(own, 0).wait_recv()
-
-    @pl.when(slab == 0)
-    def _():
-        @pl.loop(0, chunks)
-        def _(c):
-            ext[c, :, 0:HW_MAX, :] = jnp.zeros((MOMENTS, HW_MAX, LANES), jnp.float32)
-
-    @pl.when(slab == slabs - 1)
-    def _():
-        @pl.loop(0, chunks)
-        def _(c):
-            ext[c, :, HW_MAX + rows :, :] = jnp.zeros((MOMENTS, HW_MAX, LANES), jnp.float32)
 
     def set_rest():
+        out_ref[MOMENTS - LATE :, :, LANES : 2 * LANES] = jnp.zeros((LATE, rows, LANES), jnp.float32)
         pieces[:, :, 0:LANES] = jnp.zeros(pieces.shape[:2] + (LANES,), jnp.bfloat16)
         pieces[:, :, LANES + all_cols :] = jnp.zeros(pieces.shape[:2] + (LANES,), jnp.bfloat16)
         for offset in range(1, chans):
@@ -342,14 +428,18 @@
             divisor = weight_total * (2 * reach + 1).astype(jnp.float32)
             scale[k] = 1.0 / divisor
 
+    def fetch(tile):
+        if not (isinstance(tile, int) and tile >= chunks):
+            drain(beams.at[tile], load_sem.at[tile - FIRST])
+
     def iteration(c, ahead, behind):
         jobs = []
         if ahead is not None:
-            jobs = [functools.partial(make, slot, ahead) for slot in range(chans)]
-            if not (isinstance(ahead, int) and ahead == edge):
-                drain(beams.at[ahead + 1], load_sem.at[ahead + 1 - FIRST])
+            jobs = makes(ahead)
+            fetch(ahead + 2)
         for k in range(MOMENTS):
-            finish(c, k)
+            if crosses(c, k):
+                finish(c, k)
             if k < MOMENTS - 1:
                 share = -(-len(jobs) // (MOMENTS - 1 - k))
                 for job in jobs[:share]:
@@ -358,6 +448,10 @@
             elif ahead is not None:
                 for hop in range(own):
                     send_on(hop, ahead)
+            if isinstance(c, int) and c == edge and k == LATE_AT:
+                for hop in range(own):
+                    for j in range(LATE):
+                        late_copy(hop, j).start()
             if behind is not None:
                 rows_of(behind, k)
         if not (isinstance(c, int) and c == edge):
@@ -366,35 +460,37 @@
     iteration(0, 2, None)
     set_rest()
     iteration(1, 3, None)
+    for hop in range(groups):
+        late_rows(hop)
     iteration(2, 4, 0)
 
-    @pl.loop(3, edge - 2)
+    @pl.loop(3, edge - 3)
     def _(c):
         iteration(c, c + 2, c - 2)
 
+    iteration(edge - 3, edge - 1, edge - 5)
     iteration(edge - 2, edge, edge - 4)
     iteration(edge - 1, None, edge - 3)
     iteration(edge, None, edge - 2)
-
     for k in range(MOMENTS):
         rows_of(edge - 1, k)
-
-    for k in range(MOMENTS):
-        rows_of(edge, k)
-
     drain(weights.at[1:chans], w_send.at[0])
     for hop in range(groups):
         drain(sums.at[2 * hop], pass_send.at[hop])
+    for j in range(LATE):
+        late_out(j)
+    for k in range(MOMENTS):
+        rows_of(edge, k)
     for hop in range(own):
         drain(sums.at[2 * hop + 1], cross_send.at[hop])
 
     @pl.when(not_first)
     def _():
-        drain(ext.at[:, :, HW_MAX : 2 * HW_MAX], up_send.at[0])
+        drain(ext.at[:, HW_MAX : 2 * HW_MAX], up_send.at[0])
 
     @pl.when(not_last)
     def _():
-        drain(ext.at[:, :, rows : rows + HW_MAX], down_send.at[0])
+        drain(ext.at[:, rows : rows + HW_MAX], down_send.at[0])
 
 
 def body(chans, slabs, beam_images, chan_weights, freq_offsets, half_widths):
@@ -424,7 +520,8 @@
             pltpu.VMEM((chans, chunks, MOMENTS, rows, LANES), f32),
             pltpu.VMEM((groups, chunks, MOMENTS, rows, LANES), f32),
             pltpu.VMEM((groups - 1, chunks, MOMENTS, rows, LANES), f32),
-            pltpu.VMEM((chunks, MOMENTS, span, LANES), f32),
+            pltpu.VMEM((chunks * MOMENTS + (groups - 1) * LATE, span, LANES), f32),
+            pltpu.VMEM((groups, LATE, rows, LANES), f32),
             pltpu.VMEM((chans, 8, LANES), f32),
             pltpu.VMEM((MOMENTS, 8, LANES), f32),
         ],

time: 39.8 us -> 38.4 us (0.965)
  Pallas kernels: 38.6 us -> 37.2 us
    pallas_call x1, Pallas kernels: 38.6 us -> 37.2 us  [body(): pl.pallas_call(functools.partial(kernel, chans, slabs), out_shape=jax.Sha...]
where the time goes in v4:
time: 38.4 us; the launch traced here: 38.2 us
  Pallas kernels  37.2 us (97%)
  local copies, waits for them, and re-layouts  1.06 us (3%)
    pallas_call x1, Pallas kernels, body(): pl.pallas_call(functools.partial(kernel, chans, slabs), out_shape=jax.Sha...  37.2 us
    unnamed x1, local copies, waits for them, and re-layouts  1.06 us

profile of v4, /device:TPU:0, one launch (start us, length us, event | category | flops | bytes accessed | tf_op | source)
XLA Modules:
  0.0 38.2 jit_solution(14208234505778988241)
XLA Ops:
  0.0 37.2 %shard_map.46 = f32[5,64,1024]{2,1,0:T(8,128)S(1)} custom-call(s32[16]{0:T(128)} %refs_0_.1, f32[16]{0:T(128)} %refs_1_.1, s32[5]{0:T(128)} %refs_2_.1, f32[16,64,4096]{2,1,0:T(8,128)} %refs_3_.1), custom_call_target="tpu_custom_call" | custom-call | tf_op jit(solution)/shard_map/pallas_call | solution.py:507
  37.2 1.1 %copy.6 = f32[5,64,1024]{2,1,0:T(8,128)} copy(f32[5,64,1024]{2,1,0:T(8,128)S(1)} %shard_map.46) | data formatting | bytes 2621440

commit v5 on v4

--- a/solution.py
+++ b/solution.py
@@ -13,9 +13,10 @@
 HALF = LANES // 2
 PARTS = 2
 ROWS_AT_ONCE = 32
-FIRST = 2
-LATE = 2
-LATE_AT = 3
+FIRST = 3
+LATE = 3
+LATE_AT = 2
+TAIL = 1
 HALVES = 2
 MESH = pl.DeviceIdType.MESH
 
@@ -106,9 +107,11 @@
     ]
     for copy in small:
         copy.start()
-    for slot in range(chans):
-        for tile in range(FIRST):
-            load(slot, tile).start()
+    for slots in (range(2 * own), range(2 * own, chans)):
+        for tiles in (range(2), range(2, FIRST)):
+            for slot in slots:
+                for tile in tiles:
+                    load(slot, tile).start()
 
     @pl.loop(FIRST, chunks)
     def _(tile):
@@ -338,7 +341,7 @@
             late_copy(hop, j).wait_recv()
             summed = summed + crossed[hop, 0, k]
         summed = summed * scale[k, 0:1, :]
-        out_ref[k, :, 0:LANES] = summed
+        out_ref[k, :, 0:LANES] = jnp.where(left, out_ref[k, :, 0:LANES], summed)
         out_ref[k, :, LANES : 2 * LANES] = jnp.where(
             left, summed, out_ref[k, :, LANES : 2 * LANES]
         )
@@ -355,26 +358,22 @@
         def _(at):
             ext[at, HW_MAX + rows :, :] = jnp.zeros((HW_MAX, LANES), jnp.float32)
 
-    for tile in range(FIRST):
-        load(0, tile).wait()
-        moments_of(0, tile)
+    def fetch(tile):
+        if not (isinstance(tile, int) and tile >= chunks):
+            drain(beams.at[tile], load_sem.at[tile - FIRST])
+
+    def now(*tiles):
+        for slot, tile in tiles:
+            load(slot, tile).wait()
+        return tiles
+
+    for tile in range(2):
+        moments_of(*now((0, tile))[0])
     columns_of(0, 0)
     pl.semaphore_wait(
         barrier, chans - 1 + not_first.astype(jnp.int32) + not_last.astype(jnp.int32)
     )
     pass_copy(0, 0).start()
-    for slot in range(1, 2 * own):
-        for tile in range(FIRST):
-            load(slot, tile).wait()
-            if slot % 2 == 1 or tile > 0:
-                moments_of(slot, tile)
-        if slot % 2 == 1:
-            load(slot + 1, 0).wait()
-            make(slot, 0, ((slot + 1, 0),))
-            send_on(slot // 2, 0)
-        else:
-            make(slot, 0)
-
     total = w_ref[0].astype(jnp.float32)
     for chan in range(1, local_chans):
         total = total + w_ref[chan].astype(jnp.float32)
@@ -382,27 +381,32 @@
     for offset in range(1, chans):
         weight_copy(offset).start()
 
-    load(2 * own, 1).wait()
-    moments_of(2 * own, 1)
-    for tile in range(FIRST):
-        load(chans - 1, tile).wait()
-    make(2 * own, 0, tuple((chans - 1, tile) for tile in range(FIRST)))
-    drain(beams.at[FIRST], load_sem.at[0])
-    make(chans - 1, 0, ((0, FIRST),))
-    jobs = makes(1)
-    for job in jobs[:-1]:
-        job()
+    for slot in range(1, 2 * own):
+        for tile in range(2):
+            moments_of(*now((slot, tile))[0])
+        make(slot, 0, now((slot - 1, 2)))
+        if slot % 2 == 1:
+            send_on(slot // 2, 0)
+    for slot in range(2 * own - 1):
+        make(slot, 1, now((slot + 1, 2)) if slot == 2 * own - 2 else ())
+    make(2 * own - 1, 1, now((2 * own, 0)))
+    moments_of(*now((2 * own, 1))[0])
+    make(2 * own, 0, now((chans - 1, 0), (chans - 1, 1)))
+    for hop in range(own):
+        send_on(hop, 1)
+    make(chans - 1, 0, now((2 * own, 2)))
+    make(2 * own, 1, now((chans - 1, 2)))
+    fetch(3)
+    make(chans - 1, 1, ((0, 3),))
     pass_copy(own, 0).wait_recv()
     for j in range(LATE):
         k = MOMENTS - LATE + j
         share(late_place(own, j), sums[chans - 1, 0, k] + passed[own, 0, k])
-    drain(beams.at[FIRST + 1], load_sem.at[1])
-    jobs[-1]()
-    for hop in range(own):
-        send_on(hop, 1)
 
     def set_rest():
-        out_ref[MOMENTS - LATE :, :, LANES : 2 * LANES] = jnp.zeros((LATE, rows, LANES), jnp.float32)
+        out_ref[MOMENTS - LATE :, :, 0 : 2 * LANES] = jnp.zeros(
+            (LATE, rows, 2 * LANES), jnp.float32
+        )
         pieces[:, :, 0:LANES] = jnp.zeros(pieces.shape[:2] + (LANES,), jnp.bfloat16)
         pieces[:, :, LANES + all_cols :] = jnp.zeros(pieces.shape[:2] + (LANES,), jnp.bfloat16)
         for offset in range(1, chans):
@@ -427,10 +431,6 @@
                 row_band[k, :, part * span : (part + 1) * span] = near
             divisor = weight_total * (2 * reach + 1).astype(jnp.float32)
             scale[k] = 1.0 / divisor
-
-    def fetch(tile):
-        if not (isinstance(tile, int) and tile >= chunks):
-            drain(beams.at[tile], load_sem.at[tile - FIRST])
 
     def iteration(c, ahead, behind):
         jobs = []
@@ -477,9 +477,11 @@
     drain(weights.at[1:chans], w_send.at[0])
     for hop in range(groups):
         drain(sums.at[2 * hop], pass_send.at[hop])
+    for k in range(MOMENTS - TAIL):
+        rows_of(edge, k)
     for j in range(LATE):
         late_out(j)
-    for k in range(MOMENTS):
+    for k in range(MOMENTS - TAIL, MOMENTS):
         rows_of(edge, k)
     for hop in range(own):
         drain(sums.at[2 * hop + 1], cross_send.at[hop])

time: 38.4 us -> 37.5 us (0.977)
  Pallas kernels: 37.2 us -> 36.2 us
    pallas_call x1, Pallas kernels: 37.2 us -> 36.2 us  [body(): pl.pallas_call(functools.partial(kernel, chans, slabs), out_shape=jax.Sha...]
where the time goes in v5:
time: 37.5 us; the launch traced here: 37.3 us
  Pallas kernels  36.2 us (97%)
  local copies, waits for them, and re-layouts  1.06 us (3%)
    pallas_call x1, Pallas kernels, body(): pl.pallas_call(functools.partial(kernel, chans, slabs), out_shape=jax.Sha...  36.2 us
    unnamed x1, local copies, waits for them, and re-layouts  1.06 us

profile of v5, /device:TPU:0, one launch (start us, length us, event | category | flops | bytes accessed | tf_op | source)
XLA Modules:
  0.0 37.3 jit_solution(2793241700304465344)
XLA Ops:
  0.0 36.2 %shard_map.46 = f32[5,64,1024]{2,1,0:T(8,128)S(1)} custom-call(s32[16]{0:T(128)} %refs_0_.1, f32[16]{0:T(128)} %refs_1_.1, s32[5]{0:T(128)} %refs_2_.1, f32[16,64,4096]{2,1,0:T(8,128)} %refs_3_.1), custom_call_target="tpu_custom_call" | custom-call | tf_op jit(solution)/shard_map/pallas_call | solution.py:509
  36.2 1.1 %copy.6 = f32[5,64,1024]{2,1,0:T(8,128)} copy(f32[5,64,1024]{2,1,0:T(8,128)S(1)} %shard_map.46) | data formatting | bytes 2621440

commit v6 on v5

--- a/solution.py
+++ b/solution.py
@@ -391,17 +391,18 @@
         make(slot, 1, now((slot + 1, 2)) if slot == 2 * own - 2 else ())
     make(2 * own - 1, 1, now((2 * own, 0)))
     moments_of(*now((2 * own, 1))[0])
-    make(2 * own, 0, now((chans - 1, 0), (chans - 1, 1)))
+    make(2 * own, 0, now((chans - 1, 0)))
+    moments_of(*now((chans - 1, 1))[0])
     for hop in range(own):
         send_on(hop, 1)
     make(chans - 1, 0, now((2 * own, 2)))
     make(2 * own, 1, now((chans - 1, 2)))
     fetch(3)
-    make(chans - 1, 1, ((0, 3),))
     pass_copy(own, 0).wait_recv()
     for j in range(LATE):
         k = MOMENTS - LATE + j
         share(late_place(own, j), sums[chans - 1, 0, k] + passed[own, 0, k])
+    make(chans - 1, 1, ((0, 3),))
 
     def set_rest():
         out_ref[MOMENTS - LATE :, :, 0 : 2 * LANES] = jnp.zeros(

time: 37.5 us -> 37.4 us (level)
  no operation moved by 1% of the time
where the time goes in v6:
time: 37.4 us; the launch traced here: 37.3 us
  Pallas kernels  36.2 us (97%)
  local copies, waits for them, and re-layouts  1.06 us (3%)
    pallas_call x1, Pallas kernels, body(): pl.pallas_call(functools.partial(kernel, chans, slabs), out_shape=jax.Sha...  36.2 us
    unnamed x1, local copies, waits for them, and re-layouts  1.06 us

profile of v6, /device:TPU:0, one launch (start us, length us, event | category | flops | bytes accessed | tf_op | source)
XLA Modules:
  0.0 37.3 jit_solution(11008348238158192160)
XLA Ops:
  0.0 36.2 %shard_map.46 = f32[5,64,1024]{2,1,0:T(8,128)S(1)} custom-call(s32[16]{0:T(128)} %refs_0_.1, f32[16]{0:T(128)} %refs_1_.1, s32[5]{0:T(128)} %refs_2_.1, f32[16,64,4096]{2,1,0:T(8,128)} %refs_3_.1), custom_call_target="tpu_custom_call" | custom-call | tf_op jit(solution)/shard_map/pallas_call | solution.py:510
  36.2 1.1 %copy.6 = f32[5,64,1024]{2,1,0:T(8,128)} copy(f32[5,64,1024]{2,1,0:T(8,128)S(1)} %shard_map.46) | data formatting | bytes 2621440
